TPU v7x, 32 devices: a whole 2x2x4 slice. The times are simulated.
32 devices in a mesh: rep: 4 (over z), own: 8 (over y, x, core).
Axes of the slice: x: 2, y: 2, z: 4, core: 2. Of those that a mesh axis runs over, the one named last changes fastest.
Arguments:
- inputs: bfloat16 [8192, 8192], P(('rep', 'own')), may hold values from -6 to 6
- cotangent: bfloat16 [8192, 8192], P(('rep', 'own')), may hold values from -6 to 6
- gate: float32 [8192], P(('rep', 'own')), may hold values from 0.05 to 0.95
- down_weight: bfloat16 [8192, 256], P('rep'), may hold values from -0.0625 to 0.0625
- up_weight: bfloat16 [8192, 256], P('rep'), may hold values from -0.0625 to 0.0625
- mixing: bfloat16 [256, 256], replicated, may hold values from -0.375 to 0.375
- owner_table: int32 [8, 8], replicated, may hold values from -1 to 31, as said below
- left_factor: float32 [64, 256, 256], P('own'), as said below
- right_factor: float32 [64, 256, 256], P('own'), as said below
Outputs:
- preconditioned: float32 [16384, 256], P('own')
Inputs may be any that keep to these rules, and one draw needn't show every extreme that they name: `owner_table`: each of the 32 block ids stands in exactly one slot; -1 marks an empty slot; some owner has all 8 slots filled. `left_factor`: every slot's matrix is symmetric positive definite. `right_factor`: every slot's matrix is symmetric positive definite.
All inputs are finite; a program needn't handle non-finite values.
Results may differ from a plain program's by a relative error of at most 0.0077.
Values may be sent and summed in bfloat16 or wider, within the bound.
No kernel may reach another device: no remote copies, remote signals or barrier semaphores. Data moves between devices by JAX's collectives and lax.ppermute only.
A program may use at most 128 MiB of HBM per device.

v0:
```python
import jax
import jax.numpy as jnp
from jax import lax
from jax.sharding import PartitionSpec as P

R = 256
ITERS = 5
BETA = 0.95
EPS = 1e-06


def batched(left, right):
    return jnp.einsum("kij,kjl->kil", left, right, precision=lax.Precision.HIGHEST)


def inverse_root(matrices):
    width = matrices.shape[-1]
    identity = jnp.eye(width, dtype=jnp.float32)
    shifted = matrices + EPS * identity
    norm_size = jnp.sqrt(jnp.sum(shifted * shifted, axis=(1, 2)))
    result = jnp.broadcast_to(identity, shifted.shape) * (norm_size ** (-0.25))[:, None, None]
    normed = shifted / norm_size[:, None, None]
    for sweep in range(ITERS):
        factor = (5.0 * identity - normed) / 4.0
        result = batched(result, factor)
        square = batched(factor, factor)
        normed = batched(batched(square, square), normed)
    return result


def shards(
    inputs, cotangent, gate, down_weight, up_weight, mixing, owner_table, left_factor, right_factor
):
    token_total = inputs.shape[0] * lax.axis_size("rep") * lax.axis_size("own")
    slot_count = left_factor.shape[0]
    lifted = (gate[:, None] * inputs.astype(jnp.float32) * cotangent.astype(jnp.float32)).astype(
        jnp.bfloat16
    )
    columns = inputs
    projected = jnp.dot(
        columns,
        lax.all_gather(down_weight, "rep", axis=0, tiled=True),
        preferred_element_type=jnp.float32,
    )
    back_proj = jnp.dot(
        lifted,
        lax.all_gather(up_weight, "rep", axis=0, tiled=True),
        preferred_element_type=jnp.float32,
    )
    inner_act = jnp.tanh(projected).astype(jnp.bfloat16)
    outer_act = jnp.tanh(jnp.dot(inner_act, mixing, preferred_element_type=jnp.float32))
    outer_slope = (back_proj * (1.0 - outer_act * outer_act)).astype(jnp.bfloat16)
    through = lax.dot_general(
        outer_slope, mixing, (((1,), (1,)), ((), ())), preferred_element_type=jnp.float32
    )
    inner_wide = inner_act.astype(jnp.float32)
    signal = (through * (1.0 - inner_wide * inner_wide)).astype(jnp.bfloat16)
    columns = inputs
    shard = lax.psum_scatter(
        lax.dot_general(
            columns, signal, (((0,), (0,)), ((), ())), preferred_element_type=jnp.float32
        )
        / token_total,
        "own",
        scatter_dimension=0,
        tiled=True,
    )
    shard = lax.psum(shard, "rep")
    my_blocks = lax.dynamic_index_in_dim(owner_table, lax.axis_index("own"), 0, keepdims=False)
    wanted = (
        jnp.maximum(my_blocks, 0)[:, None] * R + jnp.arange(R, dtype=jnp.int32)[None, :]
    ).reshape(-1)
    shard_rows = lax.all_gather(shard, "own", axis=0, tiled=True)
    row_total = shard_rows.shape[0]
    inside = (wanted >= 0) & (wanted < row_total)
    selected = jnp.take(shard_rows, jnp.clip(wanted, 0, row_total - 1), axis=0)
    owned = jnp.where(inside[:, None], selected, jnp.zeros((slot_count * R, R), jnp.float32))
    my_row = lax.dynamic_index_in_dim(owner_table, lax.axis_index("own"), 0, keepdims=False)
    filled_slots = (my_row >= 0)[:, None, None]
    gradients = jnp.where(filled_slots, owned.reshape(slot_count, R, R), 0.0)
    flipped = jnp.swapaxes(gradients, 1, 2)
    left_new = BETA * left_factor + (1.0 - BETA) * batched(gradients, flipped)
    right_new = BETA * right_factor + (1.0 - BETA) * batched(flipped, gradients)
    factors = jnp.concatenate([left_new, right_new], axis=0)
    inverse_roots = inverse_root(factors)
    preconditioned = batched(
        batched(inverse_roots[:slot_count], gradients), inverse_roots[slot_count:]
    )
    return jnp.where(filled_slots, preconditioned, 0.0).reshape(slot_count * R, R)


def solution(mesh):
    in_specs = (
        P(("rep", "own"), None),
        P(("rep", "own"), None),
        P(("rep", "own")),
        P("rep", None),
        P("rep", None),
        P(),
        P(),
        P("own", None, None),
        P("own", None, None),
    )
    out_specs = P("own", None)
    return jax.shard_map(shards, mesh=mesh, in_specs=in_specs, out_specs=out_specs, check_vma=False)
```

profile of v0, /device:TPU:0, one launch (start us, length us, event | category | flops | bytes accessed | tf_op | source)
XLA Modules:
  0.0 500.8 jit_solution(6470604852635249459)
XLA Ops:
  6.5 0.0 copy-start
  6.5 0.0 all-gather.6.cloned.1.call-start
  6.5 0.7 all-gather.6.cloned.1.call-update
  7.3 0.0 all-gather.4.cloned.1.call-start
  7.3 0.7 all-gather.4.cloned.1.call-update
  8.0 0.0 copy-start.3
  8.0 0.0 reduce-scatter.2.cloned.1.call-start
  8.1 84.3 %all-gather.6.cloned.1.call-done = bf16[8192,256]{1,0:T(8,128)(2,1)} async-done(((bf16[2048,256]{1,0:T(8,128)(2,1)}), bf16[8192,256]{1,0:T(8,128)(2,1)}) %all-gather.6.cloned.1.call-update) | async-done | bytes 4194320 | tf_op jit(solution)/shard_map/all_gather | solution.py:42
  92.4 4.7 fusion.47
  97.1 76.1 %all-gather.4.cloned.1.call-done = bf16[8192,256]{1,0:T(8,128)(2,1)} async-done(((bf16[2048,256]{1,0:T(8,128)(2,1)}), bf16[8192,256]{1,0:T(8,128)(2,1)}) %all-gather.4.cloned.1.call-update) | async-done | bytes 4194320 | tf_op jit(solution)/shard_map/all_gather | solution.py:47
  173.2 0.0 copy-done.3
  173.2 6.1 %fusion.1 = f32[256,256]{1,0:T(8,128)S(1)} fusion(bf16[8192,256]{1,0:T(8,128)(2,1)} %all-gather.4.cloned.1.call-done, bf16[256,8192]{1,0:T(8,128)(2,1)} %param.10, bf16[256,8192]{1,0:T(8,128)(2,1)} %param.9, f32[256]{0:T(256)S(1)} %copy-done.3), kind=kOutput, calls=%fused_computation.4 | convolution fusion | flops 1084227584 | bytes 12846080 | tf_op jit(solution)/shard_map/dot_general | solution.py:45
  179.3 0.0 copy-done
  179.4 0.3 fusion.46
  179.7 6.7 %fusion = f32[8192,256]{0,1:T(8,128)} fusion(bf16[256,256]{1,0:T(8,128)(2,1)S(1)} %fusion.46, bf16[256,8192]{1,0:T(8,128)(2,1)} %param.9), kind=kOutput, calls=%fused_computation.2 | convolution fusion | flops 1075838976 | bytes 12713984 | tf_op jit(solution)/shard_map/dot_general | solution.py:60
  186.4 0.0 reduce-scatter.2.cloned.1.call-update
  186.4 0.0 all-reduce.2.cloned.1.call-start
  186.5 70.0 %reduce-scatter.2.cloned.1.call-done = f32[1024,256]{0,1:T(8,128)} async-done(((f32[8192,256]{0,1:T(8,128)}), f32[1024,256]{0,1:T(8,128)}) %reduce-scatter.2.cloned.1.call-update) | async-done | bytes 1048592 | tf_op jit(solution)/shard_map/reduce_scatter | solution.py:59
  256.5 0.0 all-reduce.2.cloned.1.call-update
  256.5 0.0 all-gather.8.cloned.1.call-start
  256.5 54.1 %all-reduce.2.cloned.1.call-done = f32[1024,256]{0,1:T(8,128)} async-done(((f32[1024,256]{0,1:T(8,128)}), f32[1024,256]{0,1:T(8,128)}) %all-reduce.2.cloned.1.call-update) | async-done | bytes 1048592 | tf_op jit(solution)/shard_map/psum | solution.py:68
  310.6 0.0 all-gather.8.cloned.1.call-update
  310.6 0.7 multiply_bitcast_fusion
  311.3 0.1 fusion.70
  311.4 0.7 compare_bitcast_fusion
  312.2 0.1 fusion.74
  312.3 53.6 %all-gather.8.cloned.1.call-done = f32[8192,256]{0,1:T(8,128)} async-done(((f32[1024,256]{0,1:T(8,128)}), f32[8192,256]{0,1:T(8,128)}) %all-gather.8.cloned.1.call-update) | async-done | bytes 8388624 | tf_op jit(solution)/shard_map/all_gather | solution.py:73
  365.9 9.0 %copy.10 = f32[8192,256]{1,0:T(8,128)} copy(f32[8192,256]{0,1:T(8,128)} %all-gather.8.cloned.1.call-done) | data formatting | bytes 16777216 | tf_op jit(solution)/shard_map/all_gather | solution.py:73
  374.9 10.0 %gather_fusion = f32[2048,256]{1,0:T(8,128)S(1)} fusion(f32[8192,256]{1,0:T(8,128)} %copy.10, s32[2048]{0:T(1024)S(1)} %broadcast_clamp_fusion), kind=kCustom, calls=%fused_computation | custom fusion | bytes 4202496 | tf_op jit(solution)/shard_map/jit(_take)/gather | solution.py:76
  384.9 0.0 copy-start.2
  384.9 6.5 %multiply_add_fusion = f32[8,256,256]{2,1,0:T(8,128)S(1)} fusion(f32[8,256,256]{2,1,0:T(8,128)} %param.17, f32[8,256,256]{2,1,0:T(8,128)S(1)} %bitcast.43, pred[8]{0:T(512)(128)(4,1)S(1)} %compare_bitcast_fusion, pred[8,256]{1,0:T(8,128)(4,1)S(1)} %get-tuple-element.8, pred[8,256]{1,0:T(8,128)(4,1)S(1)} %get-tuple-element.7), kind=kOutput, calls=%fused_computation.46 | convolution fusion | flops 1613758464 | bytes 6295560 | tf_op jit(solution)/shard_map/kij,kjl->kil/dot_general | solution.py:13
  391.4 0.0 copy-done.2
  391.4 4.4 multiply_add_fusion.1
  395.8 0.6 multiply_reduce_fusion
  396.5 6.1 %fusion.8 = f32[16,256,256]{2,1,0:T(8,128)S(1)} fusion(f32[256,256]{1,0:T(8,128)S(1)} %get-tuple-element.9, f32[8,256,256]{2,1,0:T(8,128)S(1)} %multiply_add_fusion, f32[8,256,256]{2,1,0:T(8,128)S(1)} %multiply_add_fusion.1, f32[16]{0:T(128)S(1)} %get-tuple-element.5, f32[256,256]{1,0:T(8,128)S(1)} %get-tuple-element.10), kind=kOutput, calls=%fused_computation.17 | convolution fusion | flops 3226468352 | bytes 8912960 | tf_op jit(solution)/shard_map/kij,kjl->kil/dot_general | solution.py:13
  402.6 5.1 %fusion.96 = f32[16,256,256]{2,1,0:T(8,128)S(1)} fusion(f32[16,256,256]{2,1,0:T(8,128)S(1)} %fusion.8), kind=kOutput, calls=%fused_computation.115 | convolution fusion | flops 3221225472 | bytes 8388608 | tf_op jit(solution)/shard_map/kij,kjl->kil/dot_general | solution.py:13
  407.7 5.4 %fusion.92 = f32[16,256,256]{2,1,0:T(8,128)S(1)} fusion(f32[16,256,256]{2,1,0:T(8,128)S(1)} %fusion.96, f32[8,256,256]{2,1,0:T(8,128)S(1)} %multiply_add_fusion, f32[8,256,256]{2,1,0:T(8,128)S(1)} %multiply_add_fusion.1, f32[16]{0:T(128)S(1)} %get-tuple-element.5, f32[256,256]{1,0:T(8,128)S(1)} %get-tuple-element.10), kind=kOutput, calls=%fused_computation.113 | convolution fusion | flops 3224371200 | bytes 12845120 | tf_op jit(solution)/shard_map/kij,kjl->kil/dot_general | solution.py:13
  413.1 5.7 %fusion.9 = f32[16,256,256]{2,1,0:T(8,128)S(1)} fusion(f32[16,256,256]{2,1,0:T(8,128)S(1)} %fusion.92, f32[256,256]{1,0:T(8,128)S(1)} %get-tuple-element.9), kind=kOutput, calls=%fused_computation.18 | convolution fusion | flops 3223322624 | bytes 8650752 | tf_op jit(solution)/shard_map/kij,kjl->kil/dot_general | solution.py:13
  418.8 6.0 %fusion.5 = f32[16,256,256]{2,1,0:T(8,128)S(1)} fusion(f32[256,256]{1,0:T(8,128)S(1)} %get-tuple-element.9, f32[16]{0:T(128)S(1)} %get-tuple-element.6, f32[256,256]{1,0:T(8,128)S(1)} %fusion.65, f32[8,256,256]{2,1,0:T(8,128)S(1)} %multiply_add_fusion, f32[8,256,256]{2,1,0:T(8,128)S(1)} %multiply_add_fusion.1, f32[16]{0:T(128)S(1)} %get-tuple-element.5, ...), kind=kOutput, calls=%fused_computation.13 | convolution fusion | flops 3227516928 | bytes 9175168 | tf_op jit(solution)/shard_map/kij,kjl->kil/dot_general | solution.py:13
  424.8 5.3 %fusion.10 = f32[16,256,256]{2,1,0:T(8,128)S(1)} fusion(f32[16,256,256]{2,1,0:T(8,128)S(1)} %fusion.5, f32[16,256,256]{2,1,0:T(8,128)S(1)} %fusion.92, f32[256,256]{1,0:T(8,128)S(1)} %get-tuple-element.9), kind=kOutput, calls=%fused_computation.19 | convolution fusion | flops 3223322624 | bytes 12845056 | tf_op jit(solution)/shard_map/kij,kjl->kil/dot_general | solution.py:13
  430.1 5.1 %fusion.97 = f32[16,256,256]{2,1,0:T(8,128)S(1)} fusion(f32[16,256,256]{2,1,0:T(8,128)S(1)} %fusion.9), kind=kOutput, calls=%fused_computation.116 | convolution fusion | flops 3221225472 | bytes 8388608 | tf_op jit(solution)/shard_map/kij,kjl->kil/dot_general | solution.py:13
  435.2 5.2 %fusion.98 = f32[16,256,256]{2,1,0:T(8,128)S(1)} fusion(f32[16,256,256]{2,1,0:T(8,128)S(1)} %fusion.97, f32[16,256,256]{2,1,0:T(8,128)S(1)} %fusion.92), kind=kOutput, calls=%fused_computation.117 | convolution fusion | flops 3221225472 | bytes 12582912 | tf_op jit(solution)/shard_map/kij,kjl->kil/dot_general | solution.py:13
  440.4 5.6 %fusion.11 = f32[16,256,256]{2,1,0:T(8,128)S(1)} fusion(f32[16,256,256]{2,1,0:T(8,128)S(1)} %fusion.98, f32[256,256]{1,0:T(8,128)S(1)} %get-tuple-element.9), kind=kOutput, calls=%fused_computation.20 | convolution fusion | flops 3223322624 | bytes 8650752 | tf_op jit(solution)/shard_map/kij,kjl->kil/dot_general | solution.py:13
  446.0 5.4 %fusion.12 = f32[16,256,256]{2,1,0:T(8,128)S(1)} fusion(f32[16,256,256]{2,1,0:T(8,128)S(1)} %fusion.10, f32[16,256,256]{2,1,0:T(8,128)S(1)} %fusion.98, f32[256,256]{1,0:T(8,128)S(1)} %get-tuple-element.9), kind=kOutput, calls=%fused_computation.21 | convolution fusion | flops 3223322624 | bytes 12845056 | tf_op jit(solution)/shard_map/kij,kjl->kil/dot_general | solution.py:13
  451.4 5.0 fusion.99
  456.4 5.0 %fusion.100 = f32[16,256,256]{2,1,0:T(8,128)S(1)} fusion(f32[16,256,256]{2,1,0:T(8,128)S(1)} %fusion.99, f32[16,256,256]{2,1,0:T(8,128)S(1)} %fusion.98), kind=kOutput, calls=%fused_computation.119 | convolution fusion | flops 3221225472 | bytes 12582912 | tf_op jit(solution)/shard_map/kij,kjl->kil/dot_general | solution.py:13
  461.4 6.0 %fusion.13 = f32[16,256,256]{2,1,0:T(8,128)S(1)} fusion(f32[16,256,256]{2,1,0:T(8,128)S(1)} %fusion.100, f32[256,256]{1,0:T(8,128)S(1)} %get-tuple-element.9), kind=kOutput, calls=%fused_computation.22 | convolution fusion | flops 3223322624 | bytes 8650752 | tf_op jit(solution)/shard_map/kij,kjl->kil/dot_general | solution.py:13
  467.4 5.1 %fusion.14 = f32[16,256,256]{2,1,0:T(8,128)S(1)} fusion(f32[16,256,256]{2,1,0:T(8,128)S(1)} %fusion.12, f32[16,256,256]{2,1,0:T(8,128)S(1)} %fusion.100, f32[256,256]{1,0:T(8,128)S(1)} %get-tuple-element.9), kind=kOutput, calls=%fused_computation.23 | convolution fusion | flops 3223322624 | bytes 12845056 | tf_op jit(solution)/shard_map/kij,kjl->kil/dot_general | solution.py:13
  472.5 5.1 %fusion.101 = f32[16,256,256]{2,1,0:T(8,128)S(1)} fusion(f32[16,256,256]{2,1,0:T(8,128)S(1)} %fusion.13), kind=kOutput, calls=%fused_computation.120 | convolution fusion | flops 3221225472 | bytes 8388608 | tf_op jit(solution)/shard_map/kij,kjl->kil/dot_general | solution.py:13
  477.6 5.0 %fusion.102 = f32[16,256,256]{2,1,0:T(8,128)S(1)} fusion(f32[16,256,256]{2,1,0:T(8,128)S(1)} %fusion.101, f32[16,256,256]{2,1,0:T(8,128)S(1)} %fusion.100), kind=kOutput, calls=%fused_computation.121 | convolution fusion | flops 3221225472 | bytes 12582912 | tf_op jit(solution)/shard_map/kij,kjl->kil/dot_general | solution.py:13
  482.7 5.1 %fusion.2 = f32[16,256,256]{2,1,0:T(8,128)S(1)} fusion(f32[16,256,256]{2,1,0:T(8,128)S(1)} %fusion.14, f32[16,256,256]{2,1,0:T(8,128)S(1)} %fusion.102, f32[256,256]{1,0:T(8,128)S(1)} %get-tuple-element.9), kind=kOutput, calls=%fused_computation.6 | convolution fusion | flops 3223322624 | bytes 12845056 | tf_op jit(solution)/shard_map/kij,kjl->kil/dot_general | solution.py:13
  487.8 0.0 copy-start.1
  487.8 2.8 fusion.41
  490.6 3.5 fusion.38
  494.1 0.0 copy-done.1
  (6 shorter events, 0.1 us)
Async XLA Ops:
  6.5 172.8 %copy-start = (bf16[256,256]{1,0:T(8,128)(2,1)S(1)}, bf16[256,256]{1,0:T(8,128)(2,1)}, u32[]{:S(2)}) copy-start(bf16[256,256]{1,0:T(8,128)(2,1)} %param.14) | copy-start | bytes 393220
  6.5 85.9 %all-gather.6.cloned.1.call-start = ((), (), s32[]{:S(2)}) async-start(), calls=%async_computation.2 | async-start | bytes 5242880 | tf_op jit(solution)/shard_map/all_gather | solution.py:42
  7.3 166.0 %all-gather.4.cloned.1.call-start = ((), (), s32[]{:S(2)}) async-start(), calls=%async_computation.1 | async-start | bytes 5242880 | tf_op jit(solution)/shard_map/all_gather | solution.py:47
  8.0 165.2 %copy-start.3 = (f32[256]{0:T(256)S(1)}, f32[256]{0:T(256)}, u32[]{:S(2)}) copy-start(f32[256]{0:T(256)} %param.11) | copy-start | bytes 3076
  8.0 248.4 %reduce-scatter.2.cloned.1.call-start = ((), (), s32[]{:S(2)}) async-start(), calls=%async_computation.3 | async-start | bytes 9437184 | tf_op jit(solution)/shard_map/reduce_scatter | solution.py:59
  186.4 124.1 %all-reduce.2.cloned.1.call-start = ((), (), s32[]{:S(2)}) async-start(), calls=%async_computation.4 | async-start | bytes 2097152 | tf_op jit(solution)/shard_map/psum | solution.py:68
  256.5 109.4 %all-gather.8.cloned.1.call-start = ((), (), s32[]{:S(2)}) async-start(), calls=%async_computation.5 | async-start | bytes 9437184 | tf_op jit(solution)/shard_map/all_gather | solution.py:73
  384.9 6.5 %copy-start.2 = (f32[8,256,256]{2,1,0:T(8,128)S(1)}, f32[8,256,256]{2,1,0:T(8,128)}, u32[]{:S(2)}) copy-start(f32[8,256,256]{2,1,0:T(8,128)} %param.16) | copy-start | bytes 6291460
  487.8 6.3 %copy-start.1 = (bf16[256,256]{1,0:T(8,128)(2,1)S(1)}, bf16[256,256]{1,0:T(8,128)(2,1)}, u32[]{:S(2)}) copy-start(bf16[256,256]{1,0:T(8,128)(2,1)} %param.14) | copy-start | bytes 393220
Sparse Core Ops, SparseCore 0:
  8.9 83.4 all-gather.5
  94.0 79.2 all-gather.3
  186.6 69.8 reduce-scatter.1
  258.7 51.8 all-reduce.1
  312.3 53.5 all-gather.7
where the time goes:
time: 507 us; the launch traced here: 501 us
  waiting for transfers between devices  340 us (67%)
  matrix products  126 us (25%)
  local copies, waits for them, and re-layouts  19 us (4%)
  between operations  13.6 us (3%)
    dot_general x21, matrix products, batched(): jnp.einsum('kij,kjl->kil', left, right, precision=lax.Precision.HIGHEST)  108 us
    all_gather x1, waiting for transfers between devices, shards(): lax.all_gather(down_weight, 'rep', axis=0, tiled=True)  84.3 us
    all_gather x1, waiting for transfers between devices, shards(): lax.all_gather(up_weight, 'rep', axis=0, tiled=True)  76.1 us
    reduce_scatter x1, waiting for transfers between devices, shards(): lax.psum_scatter(lax.dot_general(columns, signal, (((0,), (0,)), ((), ())...  70 us
    psum x1, waiting for transfers between devices, shards(): shard = lax.psum(shard, 'rep')  54.1 us
    all_gather x1, waiting for transfers between devices, shards(): shard_rows = lax.all_gather(shard, 'own', axis=0, tiled=True)  53.6 us
  transfers between devices with their start and end apart: 5, of which 5 were waited for; matrix products, arithmetic and copies ran while one was open for 1% of the time, Pallas kernels for 0%

commit v1 on v0

--- a/solution.py
+++ b/solution.py
@@ -65,7 +65,8 @@
         scatter_dimension=0,
         tiled=True,
     )
-    shard = lax.psum(shard, "rep")
+    parts = lax.all_gather(shard, "rep", axis=0, tiled=False)
+    shard = parts.sum(axis=0)
     my_blocks = lax.dynamic_index_in_dim(owner_table, lax.axis_index("own"), 0, keepdims=False)
     wanted = (
         jnp.maximum(my_blocks, 0)[:, None] * R + jnp.arange(R, dtype=jnp.int32)[None, :]

time: 507 us -> 538 us (1.061)
  waiting for transfers between devices: 340 us -> 365 us
    all_gather x0 -> x1, waiting for transfers between devices: none -> 82.1 us  [shards(): parts = lax.all_gather(shard, 'rep', axis=0, tiled=False)]
    psum x1 -> x0, waiting for transfers between devices: 54.1 us -> none  [shards(): shard = lax.psum(shard, 'rep')]
where the time goes in v1:
time: 538 us; the launch traced here: 530 us
  waiting for transfers between devices  365 us (68%)
  matrix products  126 us (23%)
  local copies, waits for them, and re-layouts  17.4 us (3%)
  between operations  13.8 us (3%)
  other arithmetic  7.01 us (1%)
    dot_general x21, matrix products, batched(): jnp.einsum('kij,kjl->kil', left, right, precision=lax.Precision.HIGHEST)  108 us
    all_gather x1, waiting for transfers between devices, shards(): lax.all_gather(down_weight, 'rep', axis=0, tiled=True)  84.3 us
    all_gather x1, waiting for transfers between devices, shards(): parts = lax.all_gather(shard, 'rep', axis=0, tiled=False)  82.1 us
    all_gather x1, waiting for transfers between devices, shards(): lax.all_gather(up_weight, 'rep', axis=0, tiled=True)  76.1 us
    reduce_scatter x1, waiting for transfers between devices, shards(): lax.psum_scatter(lax.dot_general(columns, signal, (((0,), (0,)), ((), ())...  70 us
    all_gather x1, waiting for transfers between devices, shards(): shard_rows = lax.all_gather(shard, 'own', axis=0, tiled=True)  51.2 us
  transfers between devices with their start and end apart: 5, of which 5 were waited for; matrix products, arithmetic and copies ran while one was open for 1% of the time, Pallas kernels for 0%

profile of v1, /device:TPU:0, one launch (start us, length us, event | category | flops | bytes accessed | tf_op | source)
XLA Modules:
  0.0 529.9 jit_solution(10177599287284923515)
XLA Ops:
  6.5 0.0 copy-start
  6.5 0.0 all-gather.8.cloned.1.call-start
  6.5 0.7 all-gather.8.cloned.1.call-update
  7.3 0.0 all-gather.6.cloned.1.call-start
  7.3 0.7 all-gather.6.cloned.1.call-update
  8.0 0.0 copy-start.3
  8.0 0.0 reduce-scatter.2.cloned.1.call-start
  8.1 84.3 %all-gather.8.cloned.1.call-done = bf16[8192,256]{1,0:T(8,128)(2,1)} async-done(((bf16[2048,256]{1,0:T(8,128)(2,1)}), bf16[8192,256]{1,0:T(8,128)(2,1)}) %all-gather.8.cloned.1.call-update) | async-done | bytes 4194320 | tf_op jit(solution)/shard_map/all_gather | solution.py:42
  92.4 4.7 fusion.47
  97.1 76.1 %all-gather.6.cloned.1.call-done = bf16[8192,256]{1,0:T(8,128)(2,1)} async-done(((bf16[2048,256]{1,0:T(8,128)(2,1)}), bf16[8192,256]{1,0:T(8,128)(2,1)}) %all-gather.6.cloned.1.call-update) | async-done | bytes 4194320 | tf_op jit(solution)/shard_map/all_gather | solution.py:47
  173.2 0.0 copy-done.3
  173.2 6.1 %fusion.1 = f32[256,256]{1,0:T(8,128)S(1)} fusion(bf16[8192,256]{1,0:T(8,128)(2,1)} %all-gather.6.cloned.1.call-done, bf16[256,8192]{1,0:T(8,128)(2,1)} %param.10, bf16[256,8192]{1,0:T(8,128)(2,1)} %param.9, f32[256]{0:T(256)S(1)} %copy-done.3), kind=kOutput, calls=%fused_computation.4 | convolution fusion | flops 1084227584 | bytes 12846080 | tf_op jit(solution)/shard_map/dot_general | solution.py:45
  179.3 0.0 copy-done
  179.4 0.3 fusion.46
  179.7 6.7 %fusion = f32[8192,256]{0,1:T(8,128)} fusion(bf16[256,256]{1,0:T(8,128)(2,1)S(1)} %fusion.46, bf16[256,8192]{1,0:T(8,128)(2,1)} %param.9), kind=kOutput, calls=%fused_computation.2 | convolution fusion | flops 1075838976 | bytes 12713984 | tf_op jit(solution)/shard_map/dot_general | solution.py:60
  186.4 0.0 reduce-scatter.2.cloned.1.call-update
  186.4 0.0 all-gather.12.cloned.1.call-start
  186.5 70.0 %reduce-scatter.2.cloned.1.call-done = f32[1024,256]{0,1:T(8,128)} async-done(((f32[8192,256]{0,1:T(8,128)}), f32[1024,256]{0,1:T(8,128)}) %reduce-scatter.2.cloned.1.call-update) | async-done | bytes 1048592 | tf_op jit(solution)/shard_map/reduce_scatter | solution.py:59
  256.5 0.0 all-gather.12.cloned.1.call-update
  256.5 0.0 all-gather.10.cloned.1.call-start
  256.5 82.1 %all-gather.12.cloned.1.call-done = f32[4096,256]{0,1:T(8,128)} async-done(((f32[1024,256]{0,1:T(8,128)}), f32[4096,256]{0,1:T(8,128)}) %all-gather.12.cloned.1.call-update) | async-done | bytes 4194320 | tf_op jit(solution)/shard_map/all_gather | solution.py:68
  338.7 6.0 %reshape.112 = f32[4,1024,256]{1,0,2:T(4,128)} reshape(f32[4096,256]{0,1:T(8,128)} %all-gather.12.cloned.1.call-done) | data formatting | bytes 8388608 | tf_op jit(solution)/shard_map/all_gather | solution.py:68
  344.7 4.7 reduce_sum.18
  349.5 1.3 copy.11
  350.8 0.0 all-gather.10.cloned.1.call-update
  350.8 0.7 multiply_bitcast_fusion
  351.5 0.1 fusion.70
  351.6 0.7 compare_bitcast_fusion
  352.3 0.1 fusion.74
  352.5 51.2 %all-gather.10.cloned.1.call-done = f32[8192,256]{1,0:T(8,128)} async-done(((f32[1024,256]{1,0:T(8,128)}), f32[8192,256]{1,0:T(8,128)}) %all-gather.10.cloned.1.call-update) | async-done | bytes 8388624 | tf_op jit(solution)/shard_map/all_gather | solution.py:74
  403.7 10.0 %gather_fusion = f32[2048,256]{1,0:T(8,128)S(1)} fusion(f32[8192,256]{1,0:T(8,128)} %all-gather.10.cloned.1.call-done, s32[2048]{0:T(1024)S(1)} %broadcast_clamp_fusion), kind=kCustom, calls=%fused_computation | custom fusion | bytes 4202496 | tf_op jit(solution)/shard_map/jit(_take)/gather | solution.py:77
  413.7 0.0 copy-start.2
  413.7 6.5 %multiply_add_fusion = f32[8,256,256]{2,1,0:T(8,128)S(1)} fusion(f32[8,256,256]{2,1,0:T(8,128)} %param.17, f32[8,256,256]{2,1,0:T(8,128)S(1)} %bitcast.45, pred[8]{0:T(512)(128)(4,1)S(1)} %compare_bitcast_fusion, pred[8,256]{1,0:T(8,128)(4,1)S(1)} %get-tuple-element.8, pred[8,256]{1,0:T(8,128)(4,1)S(1)} %get-tuple-element.7), kind=kOutput, calls=%fused_computation.46 | convolution fusion | flops 1613758464 | bytes 6295560 | tf_op jit(solution)/shard_map/kij,kjl->kil/dot_general | solution.py:13
  420.2 0.0 copy-done.2
  420.2 4.4 multiply_add_fusion.1
  424.7 0.6 multiply_reduce_fusion
  425.3 6.1 %fusion.8 = f32[16,256,256]{2,1,0:T(8,128)S(1)} fusion(f32[256,256]{1,0:T(8,128)S(1)} %get-tuple-element.9, f32[8,256,256]{2,1,0:T(8,128)S(1)} %multiply_add_fusion, f32[8,256,256]{2,1,0:T(8,128)S(1)} %multiply_add_fusion.1, f32[16]{0:T(128)S(1)} %get-tuple-element.5, f32[256,256]{1,0:T(8,128)S(1)} %get-tuple-element.10), kind=kOutput, calls=%fused_computation.17 | convolution fusion | flops 3226468352 | bytes 8912960 | tf_op jit(solution)/shard_map/kij,kjl->kil/dot_general | solution.py:13
  431.4 5.1 fusion.96
  436.6 5.6 %fusion.92 = f32[16,256,256]{2,1,0:T(8,128)S(1)} fusion(f32[16,256,256]{2,1,0:T(8,128)S(1)} %fusion.96, f32[8,256,256]{2,1,0:T(8,128)S(1)} %multiply_add_fusion, f32[8,256,256]{2,1,0:T(8,128)S(1)} %multiply_add_fusion.1, f32[16]{0:T(128)S(1)} %get-tuple-element.5, f32[256,256]{1,0:T(8,128)S(1)} %get-tuple-element.10), kind=kOutput, calls=%fused_computation.113 | convolution fusion | flops 3224371200 | bytes 12845120 | tf_op jit(solution)/shard_map/kij,kjl->kil/dot_general | solution.py:13
  442.2 5.7 %fusion.9 = f32[16,256,256]{2,1,0:T(8,128)S(1)} fusion(f32[16,256,256]{2,1,0:T(8,128)S(1)} %fusion.92, f32[256,256]{1,0:T(8,128)S(1)} %get-tuple-element.9), kind=kOutput, calls=%fused_computation.18 | convolution fusion | flops 3223322624 | bytes 8650752 | tf_op jit(solution)/shard_map/kij,kjl->kil/dot_general | solution.py:13
  447.8 5.8 %fusion.5 = f32[16,256,256]{2,1,0:T(8,128)S(1)} fusion(f32[256,256]{1,0:T(8,128)S(1)} %get-tuple-element.9, f32[16]{0:T(128)S(1)} %get-tuple-element.6, f32[256,256]{1,0:T(8,128)S(1)} %fusion.65, f32[8,256,256]{2,1,0:T(8,128)S(1)} %multiply_add_fusion, f32[8,256,256]{2,1,0:T(8,128)S(1)} %multiply_add_fusion.1, f32[16]{0:T(128)S(1)} %get-tuple-element.5, ...), kind=kOutput, calls=%fused_computation.13 | convolution fusion | flops 3227516928 | bytes 9175168 | tf_op jit(solution)/shard_map/kij,kjl->kil/dot_general | solution.py:13
  453.6 5.3 fusion.10
  458.9 5.1 fusion.97
  464.0 5.3 fusion.98
  469.3 5.6 %fusion.11 = f32[16,256,256]{2,1,0:T(8,128)S(1)} fusion(f32[16,256,256]{2,1,0:T(8,128)S(1)} %fusion.98, f32[256,256]{1,0:T(8,128)S(1)} %get-tuple-element.9), kind=kOutput, calls=%fused_computation.20 | convolution fusion | flops 3223322624 | bytes 8650752 | tf_op jit(solution)/shard_map/kij,kjl->kil/dot_general | solution.py:13
  474.9 5.6 %fusion.12 = f32[16,256,256]{2,1,0:T(8,128)S(1)} fusion(f32[16,256,256]{2,1,0:T(8,128)S(1)} %fusion.10, f32[16,256,256]{2,1,0:T(8,128)S(1)} %fusion.98, f32[256,256]{1,0:T(8,128)S(1)} %get-tuple-element.9), kind=kOutput, calls=%fused_computation.21 | convolution fusion | flops 3223322624 | bytes 12845056 | tf_op jit(solution)/shard_map/kij,kjl->kil/dot_general | solution.py:13
  480.5 5.0 fusion.99
  485.4 5.0 fusion.100
  490.4 5.7 %fusion.13 = f32[16,256,256]{2,1,0:T(8,128)S(1)} fusion(f32[16,256,256]{2,1,0:T(8,128)S(1)} %fusion.100, f32[256,256]{1,0:T(8,128)S(1)} %get-tuple-element.9), kind=kOutput, calls=%fused_computation.22 | convolution fusion | flops 3223322624 | bytes 8650752 | tf_op jit(solution)/shard_map/kij,kjl->kil/dot_general | solution.py:13
  496.2 5.1 fusion.14
  501.3 5.2 fusion.101
  506.5 5.0 fusion.102
  511.5 5.1 fusion.2
  516.7 0.0 copy-start.1
  516.7 2.8 fusion.41
  519.5 3.5 fusion.38
  523.0 0.0 copy-done.1
  (6 shorter events, 0.1 us)
Async XLA Ops:
  6.5 172.8 %copy-start = (bf16[256,256]{1,0:T(8,128)(2,1)S(1)}, bf16[256,256]{1,0:T(8,128)(2,1)}, u32[]{:S(2)}) copy-start(bf16[256,256]{1,0:T(8,128)(2,1)} %param.14) | copy-start | bytes 393220
  6.5 85.9 %all-gather.8.cloned.1.call-start = ((), (), s32[]{:S(2)}) async-start(), calls=%async_computation.2 | async-start | bytes 5242880 | tf_op jit(solution)/shard_map/all_gather | solution.py:42
  7.3 166.0 %all-gather.6.cloned.1.call-start = ((), (), s32[]{:S(2)}) async-start(), calls=%async_computation.1 | async-start | bytes 5242880 | tf_op jit(solution)/shard_map/all_gather | solution.py:47
  8.0 165.2 %copy-start.3 = (f32[256]{0:T(256)S(1)}, f32[256]{0:T(256)}, u32[]{:S(2)}) copy-start(f32[256]{0:T(256)} %param.11) | copy-start | bytes 3076
  8.0 248.4 %reduce-scatter.2.cloned.1.call-start = ((), (), s32[]{:S(2)}) async-start(), calls=%async_computation.3 | async-start | bytes 9437184 | tf_op jit(solution)/shard_map/reduce_scatter | solution.py:59
  186.4 152.2 %all-gather.12.cloned.1.call-start = ((), (), s32[]{:S(2)}) async-start(), calls=%async_computation.5 | async-start | bytes 5242880 | tf_op jit(solution)/shard_map/all_gather | solution.py:68
  256.5 147.2 %all-gather.10.cloned.1.call-start = ((), (), s32[]{:S(2)}) async-start(), calls=%async_computation.4 | async-start | bytes 9437184 | tf_op jit(solution)/shard_map/all_gather | solution.py:74
  413.7 6.5 %copy-start.2 = (f32[8,256,256]{2,1,0:T(8,128)S(1)}, f32[8,256,256]{2,1,0:T(8,128)}, u32[]{:S(2)}) copy-start(f32[8,256,256]{2,1,0:T(8,128)} %param.16) | copy-start | bytes 6291460
  516.7 6.3 %copy-start.1 = (bf16[256,256]{1,0:T(8,128)(2,1)S(1)}, bf16[256,256]{1,0:T(8,128)(2,1)}, u32[]{:S(2)}) copy-start(bf16[256,256]{1,0:T(8,128)(2,1)} %param.14) | copy-start | bytes 393220
Sparse Core Ops, SparseCore 0:
  8.9 83.4 all-gather.7
  94.0 79.2 all-gather.5
  186.6 69.8 reduce-scatter.1
  257.9 80.7 all-gather.11
  350.9 52.7 all-gather.9
